TPU v7x, 32 devices: a whole 2x2x4 slice. The times are simulated.
32 devices in a mesh: pb: 4 (over x, core), dev: 8 (over z, y).
Axes of the slice: x: 2, y: 2, z: 4, core: 2. Of those that a mesh axis runs over, the one named last changes fastest.
Arguments:
- queries: bfloat16 [1024, 128], P(('dev', 'pb')), may hold values from -0.75 to 0.75
- documents: bfloat16 [8192, 128], P(('pb', 'dev')), may hold values from -0.75 to 0.75
- lengths: int32 [64], P(('pb', 'dev')), may hold values from 1 to 128
- normalizers: float32 [64, 1024], P('pb', 'dev'), may hold values from 4.5 to 7.5
- probs: float32 [32, 64], P('dev', 'pb'), may hold values from 0.01 to 0.2
- positives: int32 [32], P('dev'), may hold values from 0 to 63
Outputs:
- query_grad: float32 [1024, 128], P(('dev', 'pb'))
- doc_grad: float32 [8192, 128], P(('pb', 'dev'))
Inputs may be any that keep to these rules, and one draw needn't show every extreme that they name: `lengths`: slots of a document at positions of its length or beyond are padding. `positives`: index of the query's paired document among all 64.
All inputs are finite; a program needn't handle non-finite values.
Results may differ from a plain program's by a relative error of at most 0.00082.
Values may be sent and summed in bfloat16 or wider, within the bound.
A program may use at most 64 MiB of HBM per device.

v0:
```python
import jax
import jax.numpy as jnp
from jax import lax
from jax.sharding import PartitionSpec as P

sharpness = 10.0


def shifted_2(x, axis, by):
    devices = lax.axis_size(axis)
    return lax.ppermute(x, axis, [(i, (i + by) % devices) for i in range(devices)])


def interact(query_rows, z_rows, p_cols, positive_ids, doc_rows, doc_lengths, first_doc):
    query_total = query_rows.shape[0]
    query_count = p_cols.shape[0]
    query_length = query_total // query_count
    doc_count = doc_lengths.shape[0]
    doc_length = doc_rows.shape[0] // doc_count
    scores = lax.dot_general(
        query_rows, doc_rows, (((1,), (1,)), ((), ())), preferred_element_type=jnp.float32
    )
    scores = scores.reshape(query_count, query_length, doc_count, doc_length)
    doc_ids = first_doc + jnp.arange(doc_count, dtype=jnp.int32)
    signal = p_cols - (positive_ids[:, None] == doc_ids[None, :]).astype(jnp.float32)
    present = (jnp.arange(doc_length, dtype=jnp.int32)[None, :] < doc_lengths[:, None]).astype(
        jnp.float32
    )
    z_cols = jnp.transpose(z_rows.reshape(doc_count, query_count, query_length), (1, 2, 0))
    shifted = sharpness * scores - z_cols[:, :, :, None]
    shifted = jnp.minimum(shifted, 0.0)
    weight = jnp.exp(shifted) * present[None, None] * signal[:, None, :, None]
    weight = weight.reshape(query_total, doc_count * doc_length).astype(jnp.bfloat16)
    query_part = jnp.dot(weight, doc_rows, preferred_element_type=jnp.float32)
    doc_part = lax.dot_general(
        weight, query_rows, (((0,), (0,)), ((), ())), preferred_element_type=jnp.float32
    )
    return (query_part, doc_part)


def columns(source_table, start_col, span_count):
    return lax.dynamic_slice_in_dim(source_table, start_col, span_count, 1)


def table_rows(source_table, start_row, span_count):
    return lax.dynamic_slice_in_dim(source_table, start_row, span_count, 0)


def per_device(queries, documents, lengths, normalizers, probs, positives):
    cycle_length = lax.axis_size("dev")
    cycle_place = lax.axis_index("dev")
    row_index = lax.axis_index("pb")
    doc_count = lengths.shape[0]
    gathered = lax.all_gather(queries, "pb", axis=0, tiled=True)
    query_zero = jnp.zeros((gathered.shape[0], documents.shape[1]), jnp.float32)

    def visit_block(anchor, doc_rows, doc_lengths, offset):
        span_count = doc_lengths.shape[0]
        first_doc = (row_index * cycle_length + anchor) * doc_count + offset
        return interact(
            gathered,
            table_rows(normalizers, anchor * doc_count + offset, span_count),
            columns(probs, anchor * doc_count + offset, span_count),
            positives,
            doc_rows,
            doc_lengths,
            first_doc,
        )

    def advance(rotation, carried):
        doc_rows, doc_lengths, doc_sums, query_sums = carried
        anchor = (cycle_place - rotation) % cycle_length
        query_part, doc_part = visit_block(anchor, doc_rows, doc_lengths, 0)
        moved_rows, moved_lengths = shifted_2((doc_rows, doc_lengths), "dev", 1)
        moved_sums = shifted_2(doc_sums + doc_part, "dev", 1)
        return (moved_rows, moved_lengths, moved_sums, query_sums + query_part)

    initial = (documents, lengths, jnp.zeros(documents.shape, jnp.float32), query_zero)
    doc_rows, doc_lengths, doc_sums, query_sums = lax.fori_loop(
        0, cycle_length - 1, advance, initial
    )
    anchor = (cycle_place - (cycle_length - 1)) % cycle_length
    query_part, doc_part = visit_block(anchor, doc_rows, doc_lengths, 0)
    doc_grad = shifted_2(doc_sums + doc_part, "dev", 1)
    query_sums = query_sums + query_part
    query_grad = lax.psum_scatter(query_sums, "pb", scatter_dimension=0, tiled=True)
    return (query_grad, doc_grad)


def solution(mesh):
    in_specs = (
        P(("dev", "pb"), None),
        P(("pb", "dev"), None),
        P(("pb", "dev")),
        P("pb", "dev"),
        P("dev", "pb"),
        P("dev"),
    )
    out_specs = (P(("dev", "pb"), None), P(("pb", "dev"), None))
    return jax.shard_map(
        per_device, mesh=mesh, in_specs=in_specs, out_specs=out_specs, check_vma=False
    )
```

profile of v0, /device:TPU:0, one launch (start us, length us, event | category | flops | bytes accessed | tf_op | source)
XLA Modules:
  0.0 125.6 jit_solution(14315371797168652839)
XLA Ops:
  7.2 0.7 copy-done.3
  7.9 6.2 %all_gather.3 = bf16[128,128]{1,0:T(8,128)(2,1)S(1)} all-gather(bf16[32,128]{1,0:T(8,128)(2,1)S(1)} %copy-done.3), channel_id=1, replica_groups=mesh['pb'=4,'dev'=8] {'pb'}, dimensions={0}, use_global_device_ids=true | all-gather | bytes 40960 | tf_op jit(solution)/shard_map/all_gather | solution.py:54
  14.1 0.7 copy-done.1
  15.1 0.7 constant_dynamic-slice_fusion.1
  16.0 0.2 sub.62
  16.4 0.8 copy-done
  17.2 78.5 %while.22 = (s32[]{:T(128)}, bf16[256,128]{1,0:T(8,128)(2,1)S(1)}, s32[2]{0:T(128)S(1)}, f32[256,128]{1,0:T(8,128)S(1)}, f32[128,128]{1,0:T(8,128)S(1)}, /*index...) while((s32[]{:T(128)}, bf16[256,128]{1,0:T(8,128)(2,1)S(1)}, ...), condition=%wide.region_1.2_spmd.clone, body=%wide.region_0.1_spmd.clone.sunk | while | flops 25428524 | bytes 2238114 | solution.py:79
  17.2 2.0 %collective-permute-start = (bf16[256,128]{1,0:T(8,128)(2,1)S(1)}, bf16[256,128]{1,0:T(8,128)(2,1)S(1)}, u32[]{:S(2)}, u32[]{:S(2)}) collective-permute-start(bf16[256,128]{1,0:T(8,128)(2,1)S(1)} %copy.40), channel_id=1, source_target_pairs={{0,1},{1,2},{2,3},{3,4},{4,5},{5,6},{6,7},{7,0},{8,9},{9,10},{10,1... | collective-permute-start | bytes 196616 | tf_op jit(solution)/shard_map/while/body/eval_jaxpr/ppermute | solution.py:11
  19.2 1.5 %collective-permute-start.1 = (s32[2]{0:T(128)S(1)}, s32[2]{0:T(128)S(1)}, u32[]{:S(2)}, u32[]{:S(2)}) collective-permute-start(s32[2]{0:T(128)S(1)} %copy.41), channel_id=1, source_target_pairs={{0,1},{1,2},{2,3},{3,4},{4,5},{5,6},{6,7},{7,0},{8,9},{9,10},{10,1... | collective-permute-start | bytes 32 | tf_op jit(solution)/shard_map/while/body/eval_jaxpr/ppermute | solution.py:11
  20.7 0.7 constant_dynamic-slice_fusion.3
  21.8 0.2 sub.102
  22.0 0.2 fusion.38
  22.2 0.2 convolution_add_fusion.6
  22.4 1.6 %collective-permute-start.2 = (f32[256,128]{1,0:T(8,128)S(1)}, f32[256,128]{1,0:T(8,128)S(1)}, u32[]{:S(2)}, u32[]{:S(2)}) collective-permute-start(f32[256,128]{1,0:T(8,128)S(1)} %convolution_add_fusion.6), channel_id=1, source_target_pairs={{0,1},{1,2},{2,3},{3,4},{4,5},{5,6},{6,7},{7,0},{8,9},{9,10},{10,1... | collective-permute-start | bytes 393224 | tf_op jit(solution)/shard_map/while/body/eval_jaxpr/ppermute | solution.py:11
  24.1 1.3 %collective-permute-done.1 = s32[2]{0:T(128)S(1)} collective-permute-done((s32[2]{0:T(128)S(1)}, s32[2]{0:T(128)S(1)}, u32[]{:S(2)}, u32[]{:S(2)}) %collective-permute-start.1) | collective-permute-done | bytes 40 | tf_op jit(solution)/shard_map/while/body/eval_jaxpr/ppermute | solution.py:11
  25.5 4.8 %collective-permute-done.2 = f32[256,128]{1,0:T(8,128)S(1)} collective-permute-done((f32[256,128]{1,0:T(8,128)S(1)}, f32[256,128]{1,0:T(8,128)S(1)}, u32[]{:S(2)}, u32[]{:S(2)}) %collective-permute-start.2) | collective-permute-done | bytes 131104 | tf_op jit(solution)/shard_map/while/body/eval_jaxpr/ppermute | solution.py:11
  30.3 1.2 collective-permute-start.1
  31.6 0.7 constant_dynamic-slice_fusion.3
  32.6 0.2 sub.102
  32.8 0.2 fusion.38
  33.0 0.2 convolution_add_fusion.6
  33.2 0.7 collective-permute-start.2
  34.1 3.7 %collective-permute-done.1 = s32[2]{0:T(128)S(1)} collective-permute-done((s32[2]{0:T(128)S(1)}, s32[2]{0:T(128)S(1)}, u32[]{:S(2)}, u32[]{:S(2)}) %collective-permute-start.1) | collective-permute-done | bytes 40 | tf_op jit(solution)/shard_map/while/body/eval_jaxpr/ppermute | solution.py:11
  37.7 3.2 %collective-permute-done.2 = f32[256,128]{1,0:T(8,128)S(1)} collective-permute-done((f32[256,128]{1,0:T(8,128)S(1)}, f32[256,128]{1,0:T(8,128)S(1)}, u32[]{:S(2)}, u32[]{:S(2)}) %collective-permute-start.2) | collective-permute-done | bytes 131104 | tf_op jit(solution)/shard_map/while/body/eval_jaxpr/ppermute | solution.py:11
  41.0 1.2 collective-permute-start.1
  42.2 0.7 constant_dynamic-slice_fusion.3
  43.3 0.2 sub.102
  43.5 0.2 fusion.38
  43.7 0.2 convolution_add_fusion.6
  44.1 3.9 %collective-permute-done.1 = s32[2]{0:T(128)S(1)} collective-permute-done((s32[2]{0:T(128)S(1)}, s32[2]{0:T(128)S(1)}, u32[]{:S(2)}, u32[]{:S(2)}) %collective-permute-start.1) | collective-permute-done | bytes 40 | tf_op jit(solution)/shard_map/while/body/eval_jaxpr/ppermute | solution.py:11
  48.1 3.5 %collective-permute-done.2 = f32[256,128]{1,0:T(8,128)S(1)} collective-permute-done((f32[256,128]{1,0:T(8,128)S(1)}, f32[256,128]{1,0:T(8,128)S(1)}, u32[]{:S(2)}, u32[]{:S(2)}) %collective-permute-start.2) | collective-permute-done | bytes 131104 | tf_op jit(solution)/shard_map/while/body/eval_jaxpr/ppermute | solution.py:11
  51.7 0.7 constant_dynamic-slice_fusion.3
  52.8 0.2 sub.102
  53.0 0.2 fusion.38
  53.2 0.2 convolution_add_fusion.6
  53.4 2.0 %collective-permute-start.2 = (f32[256,128]{1,0:T(8,128)S(1)}, f32[256,128]{1,0:T(8,128)S(1)}, u32[]{:S(2)}, u32[]{:S(2)}) collective-permute-start(f32[256,128]{1,0:T(8,128)S(1)} %convolution_add_fusion.6), channel_id=1, source_target_pairs={{0,1},{1,2},{2,3},{3,4},{4,5},{5,6},{6,7},{7,0},{8,9},{9,10},{10,1... | collective-permute-start | bytes 393224 | tf_op jit(solution)/shard_map/while/body/eval_jaxpr/ppermute | solution.py:11
  55.5 3.1 %collective-permute-done.1 = s32[2]{0:T(128)S(1)} collective-permute-done((s32[2]{0:T(128)S(1)}, s32[2]{0:T(128)S(1)}, u32[]{:S(2)}, u32[]{:S(2)}) %collective-permute-start.1) | collective-permute-done | bytes 40 | tf_op jit(solution)/shard_map/while/body/eval_jaxpr/ppermute | solution.py:11
  58.6 2.5 %collective-permute-done.2 = f32[256,128]{1,0:T(8,128)S(1)} collective-permute-done((f32[256,128]{1,0:T(8,128)S(1)}, f32[256,128]{1,0:T(8,128)S(1)}, u32[]{:S(2)}, u32[]{:S(2)}) %collective-permute-start.2) | collective-permute-done | bytes 131104 | tf_op jit(solution)/shard_map/while/body/eval_jaxpr/ppermute | solution.py:11
  61.3 3.3 %collective-permute-start.1 = (s32[2]{0:T(128)S(1)}, s32[2]{0:T(128)S(1)}, u32[]{:S(2)}, u32[]{:S(2)}) collective-permute-start(s32[2]{0:T(128)S(1)} %copy.41), channel_id=1, source_target_pairs={{0,1},{1,2},{2,3},{3,4},{4,5},{5,6},{6,7},{7,0},{8,9},{9,10},{10,1... | collective-permute-start | bytes 32 | tf_op jit(solution)/shard_map/while/body/eval_jaxpr/ppermute | solution.py:11
  64.6 0.7 constant_dynamic-slice_fusion.3
  65.7 0.2 sub.102
  65.9 0.2 fusion.38
  66.1 0.2 convolution_add_fusion.6
  66.6 1.6 %collective-permute-done.1 = s32[2]{0:T(128)S(1)} collective-permute-done((s32[2]{0:T(128)S(1)}, s32[2]{0:T(128)S(1)}, u32[]{:S(2)}, u32[]{:S(2)}) %collective-permute-start.1) | collective-permute-done | bytes 40 | tf_op jit(solution)/shard_map/while/body/eval_jaxpr/ppermute | solution.py:11
  68.2 6.4 %collective-permute-done.2 = f32[256,128]{1,0:T(8,128)S(1)} collective-permute-done((f32[256,128]{1,0:T(8,128)S(1)}, f32[256,128]{1,0:T(8,128)S(1)}, u32[]{:S(2)}, u32[]{:S(2)}) %collective-permute-start.2) | collective-permute-done | bytes 131104 | tf_op jit(solution)/shard_map/while/body/eval_jaxpr/ppermute | solution.py:11
  74.6 1.1 collective-permute-start.1
  75.7 0.7 constant_dynamic-slice_fusion.3
  76.8 0.2 sub.102
  77.0 0.2 fusion.38
  77.2 0.2 convolution_add_fusion.6
  77.6 4.4 %collective-permute-done.1 = s32[2]{0:T(128)S(1)} collective-permute-done((s32[2]{0:T(128)S(1)}, s32[2]{0:T(128)S(1)}, u32[]{:S(2)}, u32[]{:S(2)}) %collective-permute-start.1) | collective-permute-done | bytes 40 | tf_op jit(solution)/shard_map/while/body/eval_jaxpr/ppermute | solution.py:11
  82.0 3.6 %collective-permute-done.2 = f32[256,128]{1,0:T(8,128)S(1)} collective-permute-done((f32[256,128]{1,0:T(8,128)S(1)}, f32[256,128]{1,0:T(8,128)S(1)}, u32[]{:S(2)}, u32[]{:S(2)}) %collective-permute-start.2) | collective-permute-done | bytes 131104 | tf_op jit(solution)/shard_map/while/body/eval_jaxpr/ppermute | solution.py:11
  85.7 0.6 collective-permute-start.1
  86.3 0.7 constant_dynamic-slice_fusion.3
  87.3 0.2 sub.102
  87.5 0.2 fusion.38
  87.7 0.2 convolution_add_fusion.6
  88.2 4.7 %collective-permute-done.1 = s32[2]{0:T(128)S(1)} collective-permute-done((s32[2]{0:T(128)S(1)}, s32[2]{0:T(128)S(1)}, u32[]{:S(2)}, u32[]{:S(2)}) %collective-permute-start.1) | collective-permute-done | bytes 40 | tf_op jit(solution)/shard_map/while/body/eval_jaxpr/ppermute | solution.py:11
  92.9 2.7 %collective-permute-done.2 = f32[256,128]{1,0:T(8,128)S(1)} collective-permute-done((f32[256,128]{1,0:T(8,128)S(1)}, f32[256,128]{1,0:T(8,128)S(1)}, u32[]{:S(2)}, u32[]{:S(2)}) %collective-permute-start.2) | collective-permute-done | bytes 131104 | tf_op jit(solution)/shard_map/while/body/eval_jaxpr/ppermute | solution.py:11
  95.7 0.2 fusion.12
  96.1 0.8 convolution_add_fusion.3
  97.0 6.8 %collective-permute-done.3 = f32[256,128]{1,0:T(8,128)S(1)} collective-permute-done((f32[256,128]{1,0:T(8,128)S(1)}, f32[256,128]{1,0:T(8,128)S(1)}, u32[]{:S(2)}, u32[]{:S(2)}) %collective-permute-start.3) | collective-permute-done | bytes 131104 | tf_op jit(solution)/shard_map/ppermute | solution.py:11
  103.8 14.3 %reduce-scatter.2.cloned.1.call-done = f32[32,128]{1,0:T(8,128)} async-done(((f32[128,128]{1,0:T(8,128)}), f32[32,128]{1,0:T(8,128)}) %reduce-scatter.2.cloned.1.call-update) | async-done | bytes 16400 | tf_op jit(solution)/shard_map/reduce_scatter | solution.py:86
  118.1 0.7 copy.54
  (105 shorter events, 5.4 us)
Async XLA Ops:
  7.2 111.0 %reduce-scatter.2.cloned.1.call-start = ((), (), s32[]{:S(2)}) async-start(), calls=%async_computation.1 | async-start | bytes 81920 | tf_op jit(solution)/shard_map/reduce_scatter | solution.py:86
  7.2 0.7 copy-start.3
  14.1 0.7 copy-start.1
  14.1 0.7 copy-start.2
  16.3 0.8 copy-start
  16.3 0.8 copy-start.4
  17.2 8.3 %collective-permute-start = (bf16[256,128]{1,0:T(8,128)(2,1)S(1)}, bf16[256,128]{1,0:T(8,128)(2,1)S(1)}, u32[]{:S(2)}, u32[]{:S(2)}) collective-permute-start(bf16[256,128]{1,0:T(8,128)(2,1)S(1)} %copy.40), channel_id=1, source_target_pairs={{0,1},{1,2},{2,3},{3,4},{4,5},{5,6},{6,7},{7,0},{8,9},{9,10},{10,1... | collective-permute-start | bytes 196616 | tf_op jit(solution)/shard_map/while/body/eval_jaxpr/ppermute | solution.py:11
  19.2 6.3 %collective-permute-start.1 = (s32[2]{0:T(128)S(1)}, s32[2]{0:T(128)S(1)}, u32[]{:S(2)}, u32[]{:S(2)}) collective-permute-start(s32[2]{0:T(128)S(1)} %copy.41), channel_id=1, source_target_pairs={{0,1},{1,2},{2,3},{3,4},{4,5},{5,6},{6,7},{7,0},{8,9},{9,10},{10,1... | collective-permute-start | bytes 32 | tf_op jit(solution)/shard_map/while/body/eval_jaxpr/ppermute | solution.py:11
  22.4 7.9 %collective-permute-start.2 = (f32[256,128]{1,0:T(8,128)S(1)}, f32[256,128]{1,0:T(8,128)S(1)}, u32[]{:S(2)}, u32[]{:S(2)}) collective-permute-start(f32[256,128]{1,0:T(8,128)S(1)} %convolution_add_fusion.6), channel_id=1, source_target_pairs={{0,1},{1,2},{2,3},{3,4},{4,5},{5,6},{6,7},{7,0},{8,9},{9,10},{10,1... | collective-permute-start | bytes 393224 | tf_op jit(solution)/shard_map/while/body/eval_jaxpr/ppermute | solution.py:11
  30.3 7.4 %collective-permute-start = (bf16[256,128]{1,0:T(8,128)(2,1)S(1)}, bf16[256,128]{1,0:T(8,128)(2,1)S(1)}, u32[]{:S(2)}, u32[]{:S(2)}) collective-permute-start(bf16[256,128]{1,0:T(8,128)(2,1)S(1)} %copy.40), channel_id=1, source_target_pairs={{0,1},{1,2},{2,3},{3,4},{4,5},{5,6},{6,7},{7,0},{8,9},{9,10},{10,1... | collective-permute-start | bytes 196616 | tf_op jit(solution)/shard_map/while/body/eval_jaxpr/ppermute | solution.py:11
  30.3 7.4 %collective-permute-start.1 = (s32[2]{0:T(128)S(1)}, s32[2]{0:T(128)S(1)}, u32[]{:S(2)}, u32[]{:S(2)}) collective-permute-start(s32[2]{0:T(128)S(1)} %copy.41), channel_id=1, source_target_pairs={{0,1},{1,2},{2,3},{3,4},{4,5},{5,6},{6,7},{7,0},{8,9},{9,10},{10,1... | collective-permute-start | bytes 32 | tf_op jit(solution)/shard_map/while/body/eval_jaxpr/ppermute | solution.py:11
  33.2 7.7 %collective-permute-start.2 = (f32[256,128]{1,0:T(8,128)S(1)}, f32[256,128]{1,0:T(8,128)S(1)}, u32[]{:S(2)}, u32[]{:S(2)}) collective-permute-start(f32[256,128]{1,0:T(8,128)S(1)} %convolution_add_fusion.6), channel_id=1, source_target_pairs={{0,1},{1,2},{2,3},{3,4},{4,5},{5,6},{6,7},{7,0},{8,9},{9,10},{10,1... | collective-permute-start | bytes 393224 | tf_op jit(solution)/shard_map/while/body/eval_jaxpr/ppermute | solution.py:11
  41.0 7.1 %collective-permute-start = (bf16[256,128]{1,0:T(8,128)(2,1)S(1)}, bf16[256,128]{1,0:T(8,128)(2,1)S(1)}, u32[]{:S(2)}, u32[]{:S(2)}) collective-permute-start(bf16[256,128]{1,0:T(8,128)(2,1)S(1)} %copy.40), channel_id=1, source_target_pairs={{0,1},{1,2},{2,3},{3,4},{4,5},{5,6},{6,7},{7,0},{8,9},{9,10},{10,1... | collective-permute-start | bytes 196616 | tf_op jit(solution)/shard_map/while/body/eval_jaxpr/ppermute | solution.py:11
  41.0 7.1 %collective-permute-start.1 = (s32[2]{0:T(128)S(1)}, s32[2]{0:T(128)S(1)}, u32[]{:S(2)}, u32[]{:S(2)}) collective-permute-start(s32[2]{0:T(128)S(1)} %copy.41), channel_id=1, source_target_pairs={{0,1},{1,2},{2,3},{3,4},{4,5},{5,6},{6,7},{7,0},{8,9},{9,10},{10,1... | collective-permute-start | bytes 32 | tf_op jit(solution)/shard_map/while/body/eval_jaxpr/ppermute | solution.py:11
  43.9 7.7 %collective-permute-start.2 = (f32[256,128]{1,0:T(8,128)S(1)}, f32[256,128]{1,0:T(8,128)S(1)}, u32[]{:S(2)}, u32[]{:S(2)}) collective-permute-start(f32[256,128]{1,0:T(8,128)S(1)} %convolution_add_fusion.6), channel_id=1, source_target_pairs={{0,1},{1,2},{2,3},{3,4},{4,5},{5,6},{6,7},{7,0},{8,9},{9,10},{10,1... | collective-permute-start | bytes 393224 | tf_op jit(solution)/shard_map/while/body/eval_jaxpr/ppermute | solution.py:11
  51.6 7.1 %collective-permute-start = (bf16[256,128]{1,0:T(8,128)(2,1)S(1)}, bf16[256,128]{1,0:T(8,128)(2,1)S(1)}, u32[]{:S(2)}, u32[]{:S(2)}) collective-permute-start(bf16[256,128]{1,0:T(8,128)(2,1)S(1)} %copy.40), channel_id=1, source_target_pairs={{0,1},{1,2},{2,3},{3,4},{4,5},{5,6},{6,7},{7,0},{8,9},{9,10},{10,1... | collective-permute-start | bytes 196616 | tf_op jit(solution)/shard_map/while/body/eval_jaxpr/ppermute | solution.py:11
  51.6 7.0 %collective-permute-start.1 = (s32[2]{0:T(128)S(1)}, s32[2]{0:T(128)S(1)}, u32[]{:S(2)}, u32[]{:S(2)}) collective-permute-start(s32[2]{0:T(128)S(1)} %copy.41), channel_id=1, source_target_pairs={{0,1},{1,2},{2,3},{3,4},{4,5},{5,6},{6,7},{7,0},{8,9},{9,10},{10,1... | collective-permute-start | bytes 32 | tf_op jit(solution)/shard_map/while/body/eval_jaxpr/ppermute | solution.py:11
  53.4 7.7 %collective-permute-start.2 = (f32[256,128]{1,0:T(8,128)S(1)}, f32[256,128]{1,0:T(8,128)S(1)}, u32[]{:S(2)}, u32[]{:S(2)}) collective-permute-start(f32[256,128]{1,0:T(8,128)S(1)} %convolution_add_fusion.6), channel_id=1, source_target_pairs={{0,1},{1,2},{2,3},{3,4},{4,5},{5,6},{6,7},{7,0},{8,9},{9,10},{10,1... | collective-permute-start | bytes 393224 | tf_op jit(solution)/shard_map/while/body/eval_jaxpr/ppermute | solution.py:11
  61.1 7.1 %collective-permute-start = (bf16[256,128]{1,0:T(8,128)(2,1)S(1)}, bf16[256,128]{1,0:T(8,128)(2,1)S(1)}, u32[]{:S(2)}, u32[]{:S(2)}) collective-permute-start(bf16[256,128]{1,0:T(8,128)(2,1)S(1)} %copy.40), channel_id=1, source_target_pairs={{0,1},{1,2},{2,3},{3,4},{4,5},{5,6},{6,7},{7,0},{8,9},{9,10},{10,1... | collective-permute-start | bytes 196616 | tf_op jit(solution)/shard_map/while/body/eval_jaxpr/ppermute | solution.py:11
  61.3 6.9 %collective-permute-start.1 = (s32[2]{0:T(128)S(1)}, s32[2]{0:T(128)S(1)}, u32[]{:S(2)}, u32[]{:S(2)}) collective-permute-start(s32[2]{0:T(128)S(1)} %copy.41), channel_id=1, source_target_pairs={{0,1},{1,2},{2,3},{3,4},{4,5},{5,6},{6,7},{7,0},{8,9},{9,10},{10,1... | collective-permute-start | bytes 32 | tf_op jit(solution)/shard_map/while/body/eval_jaxpr/ppermute | solution.py:11
  66.3 8.3 %collective-permute-start.2 = (f32[256,128]{1,0:T(8,128)S(1)}, f32[256,128]{1,0:T(8,128)S(1)}, u32[]{:S(2)}, u32[]{:S(2)}) collective-permute-start(f32[256,128]{1,0:T(8,128)S(1)} %convolution_add_fusion.6), channel_id=1, source_target_pairs={{0,1},{1,2},{2,3},{3,4},{4,5},{5,6},{6,7},{7,0},{8,9},{9,10},{10,1... | collective-permute-start | bytes 393224 | tf_op jit(solution)/shard_map/while/body/eval_jaxpr/ppermute | solution.py:11
  74.6 7.4 %collective-permute-start = (bf16[256,128]{1,0:T(8,128)(2,1)S(1)}, bf16[256,128]{1,0:T(8,128)(2,1)S(1)}, u32[]{:S(2)}, u32[]{:S(2)}) collective-permute-start(bf16[256,128]{1,0:T(8,128)(2,1)S(1)} %copy.40), channel_id=1, source_target_pairs={{0,1},{1,2},{2,3},{3,4},{4,5},{5,6},{6,7},{7,0},{8,9},{9,10},{10,1... | collective-permute-start | bytes 196616 | tf_op jit(solution)/shard_map/while/body/eval_jaxpr/ppermute | solution.py:11
  74.6 7.4 %collective-permute-start.1 = (s32[2]{0:T(128)S(1)}, s32[2]{0:T(128)S(1)}, u32[]{:S(2)}, u32[]{:S(2)}) collective-permute-start(s32[2]{0:T(128)S(1)} %copy.41), channel_id=1, source_target_pairs={{0,1},{1,2},{2,3},{3,4},{4,5},{5,6},{6,7},{7,0},{8,9},{9,10},{10,1... | collective-permute-start | bytes 32 | tf_op jit(solution)/shard_map/while/body/eval_jaxpr/ppermute | solution.py:11
  77.4 8.3 %collective-permute-start.2 = (f32[256,128]{1,0:T(8,128)S(1)}, f32[256,128]{1,0:T(8,128)S(1)}, u32[]{:S(2)}, u32[]{:S(2)}) collective-permute-start(f32[256,128]{1,0:T(8,128)S(1)} %convolution_add_fusion.6), channel_id=1, source_target_pairs={{0,1},{1,2},{2,3},{3,4},{4,5},{5,6},{6,7},{7,0},{8,9},{9,10},{10,1... | collective-permute-start | bytes 393224 | tf_op jit(solution)/shard_map/while/body/eval_jaxpr/ppermute | solution.py:11
  85.7 7.3 %collective-permute-start = (bf16[256,128]{1,0:T(8,128)(2,1)S(1)}, bf16[256,128]{1,0:T(8,128)(2,1)S(1)}, u32[]{:S(2)}, u32[]{:S(2)}) collective-permute-start(bf16[256,128]{1,0:T(8,128)(2,1)S(1)} %copy.40), channel_id=1, source_target_pairs={{0,1},{1,2},{2,3},{3,4},{4,5},{5,6},{6,7},{7,0},{8,9},{9,10},{10,1... | collective-permute-start | bytes 196616 | tf_op jit(solution)/shard_map/while/body/eval_jaxpr/ppermute | solution.py:11
  85.7 7.2 %collective-permute-start.1 = (s32[2]{0:T(128)S(1)}, s32[2]{0:T(128)S(1)}, u32[]{:S(2)}, u32[]{:S(2)}) collective-permute-start(s32[2]{0:T(128)S(1)} %copy.41), channel_id=1, source_target_pairs={{0,1},{1,2},{2,3},{3,4},{4,5},{5,6},{6,7},{7,0},{8,9},{9,10},{10,1... | collective-permute-start | bytes 32 | tf_op jit(solution)/shard_map/while/body/eval_jaxpr/ppermute | solution.py:11
  87.9 7.7 %collective-permute-start.2 = (f32[256,128]{1,0:T(8,128)S(1)}, f32[256,128]{1,0:T(8,128)S(1)}, u32[]{:S(2)}, u32[]{:S(2)}) collective-permute-start(f32[256,128]{1,0:T(8,128)S(1)} %convolution_add_fusion.6), channel_id=1, source_target_pairs={{0,1},{1,2},{2,3},{3,4},{4,5},{5,6},{6,7},{7,0},{8,9},{9,10},{10,1... | collective-permute-start | bytes 393224 | tf_op jit(solution)/shard_map/while/body/eval_jaxpr/ppermute | solution.py:11
  96.1 7.7 %collective-permute-start.3 = (f32[256,128]{1,0:T(8,128)S(1)}, f32[256,128]{1,0:T(8,128)S(1)}, u32[]{:S(2)}, u32[]{:S(2)}) collective-permute-start(f32[256,128]{1,0:T(8,128)S(1)} %convolution_add_fusion.2), channel_id=1, source_target_pairs={{0,1},{1,2},{2,3},{3,4},{4,5},{5,6},{6,7},{7,0},{8,9},{9,10},{10,1... | collective-permute-start | bytes 393224 | tf_op jit(solution)/shard_map/ppermute | solution.py:11
Sparse Core Ops, SparseCore 0:
  97.1 20.9 reduce-scatter.1
where the time goes:
time: 126 us
  waiting for transfers between devices  70.7 us (56%)
  starting transfers between devices  16 us (13%)
  between operations  14.2 us (11%)
  local copies, waits for them, and re-layouts  12.6 us (10%)
  blocking collectives  6.19 us (5%)
  matrix products  4.93 us (4%)
    ppermute x22, waiting for transfers between devices, shifted_2(): lax.ppermute(x, axis, [(i, (i + by) % devices) for i in range(devices)])  56.3 us
    ppermute x22, starting transfers between devices, shifted_2(): lax.ppermute(x, axis, [(i, (i + by) % devices) for i in range(devices)])  16 us
    reduce_scatter x1, waiting for transfers between devices, per_device(): lax.psum_scatter(query_sums, 'pb', scatter_dimension=0, tiled=True)  14.3 us
    dynamic_slice x15, local copies, waits for them, and re-layouts, table_rows(): return lax.dynamic_slice_in_dim(source_table, start_row, span_count, 0)  6.35 us
    all_gather x1, blocking collectives, per_device(): gathered = lax.all_gather(queries, 'pb', axis=0, tiled=True)  6.19 us
    unnamed x13, local copies, waits for them, and re-layouts  2.85 us
  transfers between devices with their start and end apart: 23, of which 16 were waited for; matrix products, arithmetic and copies ran while one was open for 11% of the time, Pallas kernels for 0%

commit v1 on v0

v1 whole, which is shorter than its diff:
```python
import functools

import jax
import jax.numpy as jnp
from jax import lax
from jax.experimental import pallas as pl
from jax.experimental.pallas import tpu as pltpu
from jax.sharding import PartitionSpec as P

sharpness = 10.0
MESH = pl.DeviceIdType.MESH
F32 = jnp.float32


def kernel(
    n_pb,
    n_dev,
    queries,
    documents,
    lengths,
    normalizers,
    probs,
    positives,
    query_out,
    doc_out,
    q_own,
    d_own,
    z_own,
    q_all,
    d_all,
    aux_send,
    aux_recv,
    aux_turn,
    aux_all,
    doc_part,
    pair_recv,
    pair_sum,
    chip_recv,
    q_part,
    q_recv,
    in_sem,
    q_ss,
    q_rs,
    a_ss,
    a_rs,
    d_ss,
    d_rs,
    t_ss,
    t_rs,
    e_ss,
    e_rs,
    c_ss,
    c_rs,
    r_ss,
    r_rs,
):
    my_pb = lax.axis_index("pb")
    my_dev = lax.axis_index("dev")
    own_docs = lengths.shape[0]
    slots = d_own.shape[0] // own_docs
    row_docs, block = z_own.shape
    tokens = q_own.shape[0]
    block_queries = probs.shape[0]
    query_length = block // block_queries
    n_chip = n_pb // 2
    my_chip, my_core = my_pb // 2, my_pb % 2
    partner = my_chip * 2 + (1 - my_core)

    def dev_mate(step):
        return lax.rem(my_dev + step, n_dev)

    def pb_mate(step):
        return lax.rem(my_pb + step, n_pb)

    def chip_mate(step):
        return lax.rem(my_chip + step, n_chip)

    def remote(src, dst, send, recv, pb=None, dev=None):
        return pltpu.make_async_remote_copy(
            src_ref=src,
            dst_ref=dst,
            send_sem=send,
            recv_sem=recv,
            device_id=(my_pb if pb is None else pb, my_dev if dev is None else dev),
            device_id_type=MESH,
        )

    barrier = pltpu.get_barrier_semaphore()
    for step in range(1, n_dev):
        pl.semaphore_signal(
            barrier, inc=1, device_id=(my_pb, dev_mate(step)), device_id_type=MESH
        )
    for step in range(1, n_pb):
        pl.semaphore_signal(
            barrier, inc=1, device_id=(pb_mate(step), my_dev), device_id_type=MESH
        )

    loads = [
        pltpu.make_async_copy(queries, q_own, in_sem.at[0]),
        pltpu.make_async_copy(documents, d_own, in_sem.at[1]),
        pltpu.make_async_copy(normalizers, z_own, in_sem.at[2]),
    ]
    for load in loads:
        load.start()
    for load in loads:
        load.wait()

    place0 = lax.broadcasted_iota(jnp.int32, (row_docs, row_docs), 0)
    place1 = lax.broadcasted_iota(jnp.int32, (row_docs, row_docs), 1)
    doc_ids = my_pb * row_docs + lax.broadcasted_iota(jnp.int32, (row_docs, 1), 0)
    query_of = lax.broadcasted_iota(jnp.int32, (1, block), 1) // query_length
    signal = jnp.zeros((row_docs, block), F32)
    for k in range(block_queries):
        column = jnp.sum(
            jnp.where(place0 == place1, probs[k : k + 1, :], 0.0), axis=1, keepdims=True
        )
        column = column - (doc_ids == positives[k]).astype(F32)
        signal = jnp.where(query_of == k, column, signal)
    for e in range(n_dev):
        span = slice(e * own_docs, (e + 1) * own_docs)
        aux_send[e, 0:own_docs, :] = z_own[span, :]
        aux_send[e, own_docs : 2 * own_docs, :] = signal[span, :]
    aux_recv[my_dev] = aux_send[my_dev]
    q_all[my_dev] = q_own[...]

    slot = lax.broadcasted_iota(jnp.int32, (slots, 1), 0)
    for k in range(own_docs):
        span = slice(k * slots, (k + 1) * slots)
        rows = d_own[span, :].astype(F32)
        d_all[my_pb, span, :] = jnp.where(slot < lengths[k], rows, 0.0).astype(jnp.bfloat16)

    pl.semaphore_wait(barrier, n_dev - 1 + n_pb - 1)

    aux_copies, q_copies, d_copies = [], [], []
    for step in range(1, n_dev):
        mate = dev_mate(step)
        copy = remote(
            aux_send.at[mate], aux_recv.at[my_dev], a_ss.at[step], a_rs.at[step], dev=mate
        )
        copy.start()
        aux_copies.append(copy)
    for step in range(1, n_dev):
        copy = remote(q_own, q_all.at[my_dev], q_ss.at[step], q_rs.at[step], dev=dev_mate(step))
        copy.start()
        q_copies.append(copy)
    for step in range(1, n_pb):
        copy = remote(
            d_all.at[my_pb], d_all.at[my_pb], d_ss.at[step], d_rs.at[step], pb=pb_mate(step)
        )
        copy.start()
        d_copies.append(copy)

    for copy in aux_copies:
        copy.wait_recv()
    for p in range(n_pb):
        for e in range(n_dev):
            aux_turn[p, :, e * tokens : (e + 1) * tokens] = aux_recv[
                e, :, p * tokens : (p + 1) * tokens
            ]
    aux_all[my_pb] = aux_turn[my_pb]
    turn_copies = []
    for step in range(1, n_pb):
        mate = pb_mate(step)
        copy = remote(
            aux_turn.at[mate], aux_all.at[my_pb], t_ss.at[step], t_rs.at[step], pb=mate
        )
        copy.start()
        turn_copies.append(copy)

    for copy in q_copies + d_copies + turn_copies:
        copy.wait_recv()

    q_rows = q_all[...].reshape(n_dev * tokens, q_own.shape[1])

    def interact(p, total):
        d_rows = d_all[p]
        scores = lax.dot_general(
            d_rows, q_rows, (((1,), (1,)), ((), ())), preferred_element_type=F32
        )
        aux = aux_all[p]
        parts = []
        for k in range(own_docs):
            shifted = sharpness * scores[k * slots : (k + 1) * slots, :] - aux[k : k + 1, :]
            weight = jnp.exp(jnp.minimum(shifted, 0.0)) * aux[own_docs + k : own_docs + k + 1, :]
            parts.append(weight.astype(jnp.bfloat16))
        weight = jnp.concatenate(parts, axis=0)
        doc_part[p] = jnp.dot(weight, q_rows, preferred_element_type=F32)
        return total + lax.dot_general(
            weight, d_rows, (((0,), (0,)), ((), ())), preferred_element_type=F32
        )

    total = jnp.zeros((n_dev * tokens, q_own.shape[1]), F32)
    pair_copies = []

    def send_pair(step):
        copy = remote(
            doc_part.at[chip_mate(step) * 2 + (1 - my_core)],
            pair_recv.at[step],
            e_ss.at[step],
            e_rs.at[step],
            pb=partner,
        )
        copy.start()
        pair_copies.append(copy)

    if n_chip <= 2:
        for step in range(1, n_chip):
            for core in range(2):
                total = interact(chip_mate(step) * 2 + core, total)
            send_pair(step)
        for core in range(2):
            total = interact(my_chip * 2 + core, total)
        send_pair(0)
    else:
        total = lax.fori_loop(0, n_pb, interact, total)
        for step in list(range(1, n_chip)) + [0]:
            send_pair(step)
    q_part[...] = total.reshape(q_part.shape)

    out_copies = []
    for step in range(1, n_dev):
        mate = dev_mate(step)
        copy = remote(q_part.at[mate], q_recv.at[my_dev], r_ss.at[step], r_rs.at[step], dev=mate)
        copy.start()
        out_copies.append(copy)
    q_recv[my_dev] = q_part[my_dev]

    chip_copies = []
    for step in range(1, n_chip):
        pair_copies[step - 1].wait_recv()
        pair_sum[step] = doc_part[chip_mate(step) * 2 + my_core] + pair_recv[step]
        copy = remote(
            pair_sum.at[step],
            chip_recv.at[step],
            c_ss.at[step],
            c_rs.at[step],
            pb=chip_mate(step) * 2 + my_core,
        )
        copy.start()
        chip_copies.append(copy)
    pair_copies[-1].wait_recv()
    doc_total = doc_part[my_pb] + pair_recv[0]
    for step in range(1, n_chip):
        chip_copies[step - 1].wait_recv()
        doc_total = doc_total + chip_recv[step]
    for k in range(own_docs):
        span = slice(k * slots, (k + 1) * slots)
        doc_out[span, :] = jnp.where(slot < lengths[k], doc_total[span, :], 0.0)

    for copy in out_copies:
        copy.wait_recv()
    query_total = q_recv[0]
    for e in range(1, n_dev):
        query_total = query_total + q_recv[e]
    query_out[...] = query_total

    for copy in (
        aux_copies + q_copies + d_copies + turn_copies + pair_copies + out_copies + chip_copies
    ):
        copy.wait_send()


def per_device(queries, documents, lengths, normalizers, probs, positives):
    n_pb, n_dev = lax.axis_size("pb"), lax.axis_size("dev")
    tokens, width = queries.shape
    rows = documents.shape[0]
    own_docs = lengths.shape[0]
    block = normalizers.shape[1]
    n_chip = n_pb // 2
    bf16 = jnp.bfloat16
    dma = pltpu.SemaphoreType.DMA
    hbm = pl.BlockSpec(memory_space=pl.ANY)
    vmem = pl.BlockSpec(memory_space=pltpu.VMEM)
    smem = pl.BlockSpec(memory_space=pltpu.SMEM)
    return pl.pallas_call(
        functools.partial(kernel, n_pb, n_dev),
        out_shape=(
            jax.ShapeDtypeStruct((tokens, width), F32),
            jax.ShapeDtypeStruct((rows, width), F32),
        ),
        in_specs=[hbm, hbm, smem, hbm, vmem, smem],
        out_specs=(vmem, vmem),
        scratch_shapes=[
            pltpu.VMEM((tokens, width), bf16),
            pltpu.VMEM((rows, width), bf16),
            pltpu.VMEM(normalizers.shape, F32),
            pltpu.VMEM((n_dev, tokens, width), bf16),
            pltpu.VMEM((n_pb, rows, width), bf16),
            pltpu.VMEM((n_dev, 2 * own_docs, block), F32),
            pltpu.VMEM((n_dev, 2 * own_docs, block), F32),
            pltpu.VMEM((n_pb, 2 * own_docs, n_dev * tokens), F32),
            pltpu.VMEM((n_pb, 2 * own_docs, n_dev * tokens), F32),
            pltpu.VMEM((n_pb, rows, width), F32),
            pltpu.VMEM((n_chip, rows, width), F32),
            pltpu.VMEM((n_chip, rows, width), F32),
            pltpu.VMEM((n_chip, rows, width), F32),
            pltpu.VMEM((n_dev, tokens, width), F32),
            pltpu.VMEM((n_dev, tokens, width), F32),
            dma((3,)),
        ]
        + [dma((n_dev,))] * 4
        + [dma((n_pb,))] * 4
        + [dma((n_chip,))] * 4
        + [dma((n_dev,))] * 2,
        compiler_params=pltpu.CompilerParams(collective_id=0, has_side_effects=True),
    )(queries, documents, lengths, normalizers, probs, positives)


def solution(mesh):
    in_specs = (
        P(("dev", "pb"), None),
        P(("pb", "dev"), None),
        P(("pb", "dev")),
        P("pb", "dev"),
        P("dev", "pb"),
        P("dev"),
    )
    out_specs = (P(("dev", "pb"), None), P(("pb", "dev"), None))
    return jax.shard_map(
        per_device, mesh=mesh, in_specs=in_specs, out_specs=out_specs, check_vma=False
    )
```

time: 126 us -> 24.8 us (0.20)
  waiting for transfers between devices: 70.7 us -> 0 us
  Pallas kernels: 0 us -> 20.9 us
  starting transfers between devices: 16 us -> 0 us
  between operations: 14.2 us -> 0.64 us
  local copies, waits for them, and re-layouts: 12.6 us -> 2.89 us
  blocking collectives: 6.19 us -> 0 us
  matrix products: 4.93 us -> 0 us
    ppermute x22 -> x0, waiting for transfers between devices: 56.3 us -> none  [shifted_2(): lax.ppermute(x, axis, [(i, (i + by) % devices) for i in range(devices)])]
    pallas_call x0 -> x1, Pallas kernels: none -> 20.9 us  [per_device(): pl.pallas_call(functools.partial(kernel, n_pb, n_dev), out_shape=(jax.Sha...]
    ppermute x22 -> x0, starting transfers between devices: 16 us -> none  [shifted_2(): lax.ppermute(x, axis, [(i, (i + by) % devices) for i in range(devices)])]
    reduce_scatter x1 -> x0, waiting for transfers between devices: 14.3 us -> none  [per_device(): lax.psum_scatter(query_sums, 'pb', scatter_dimension=0, tiled=True)]
    dynamic_slice x15 -> x0, local copies, waits for them, and re-layouts: 6.35 us -> none  [table_rows(): return lax.dynamic_slice_in_dim(source_table, start_row, span_count, 0)]
    all_gather x1 -> x0, blocking collectives: 6.19 us -> none  [per_device(): gathered = lax.all_gather(queries, 'pb', axis=0, tiled=True)]
    dot_general x24 -> x0, matrix products: 4.93 us -> none  [the longest x8 1.91 us: interact(): query_part = jnp.dot(weight, doc_rows, preferred_element_type=jnp.float32)]
    sub x9 -> x0, local copies, waits for them, and re-layouts: 1.66 us -> none  [interact(): shifted = sharpness * scores - z_cols[:, :, :, None]]
  transfers between devices with their start and end apart: 23 -> 0, of which waited for: 16 -> 0; matrix products, arithmetic and copies ran while one was open for 11% -> 0% of each run, Pallas kernels for 0% -> 0%
where the time goes in v1:
time: 24.8 us; the launch traced here: 24.5 us
  Pallas kernels  20.9 us (84%)
  local copies, waits for them, and re-layouts  2.89 us (12%)
  between operations  0.64 us (3%)
    pallas_call x1, Pallas kernels, per_device(): pl.pallas_call(functools.partial(kernel, n_pb, n_dev), out_shape=(jax.Sha...  20.9 us
    unnamed x2, local copies, waits for them, and re-layouts  2.89 us

profile of v1, /device:TPU:0, one launch (start us, length us, event | category | flops | bytes accessed | tf_op | source)
XLA Modules:
  0.0 24.5 jit_solution(1534562435797347894)
XLA Ops:
  0.6 20.9 %shard_map.77 = (f32[32,128]{1,0:T(8,128)}, f32[256,128]{1,0:T(8,128)}) custom-call(bf16[32,128]{1,0:T(8,128)(2,1)} %queries.1, bf16[256,128]{1,0:T(8,128)(2,1)} %documents.1, s32[2]{0:T(128)} %lengths.1, f32[16,128]{1,0:T(8,128)} %normalizers.1, f32[4,16]{1,0:T(4,128)} %probs.1, s32[4]{0:T(128)} %positives.1), custom_call_target="tpu_custom_call" | custom-call | tf_op jit(solution)/shard_map/pallas_call | solution.py:275
  21.6 1.3 %copy.10 = f32[32,128]{1,0:T(8,128)} copy(f32[32,128]{1,0:T(8,128)} %get-tuple-element.4) | data formatting | bytes 32768
  22.9 1.6 %copy.11 = f32[256,128]{1,0:T(8,128)} copy(f32[256,128]{1,0:T(8,128)} %get-tuple-element.5) | data formatting | bytes 262144

commit v2 on v1

--- a/solution.py
+++ b/solution.py
@@ -17,12 +17,16 @@
     n_dev,
     queries,
     documents,
+    lengths_in,
+    normalizers,
+    probs_in,
+    positives_in,
+    query_out,
+    doc_out,
     lengths,
-    normalizers,
     probs,
     positives,
-    query_out,
-    doc_out,
+    scores,
     q_own,
     d_own,
     z_own,
@@ -66,14 +70,21 @@
     my_chip, my_core = my_pb // 2, my_pb % 2
     partner = my_chip * 2 + (1 - my_core)
 
+    def crossed(place, step, count):
+        mate, bit = 0, 1
+        while bit < count:
+            mate = mate + bit * ((place // bit + step // bit) % 2)
+            bit *= 2
+        return mate
+
     def dev_mate(step):
-        return lax.rem(my_dev + step, n_dev)
+        return crossed(my_dev, step, n_dev)
 
     def pb_mate(step):
-        return lax.rem(my_pb + step, n_pb)
+        return crossed(my_pb, step, n_pb)
 
     def chip_mate(step):
-        return lax.rem(my_chip + step, n_chip)
+        return crossed(my_chip, step, n_chip)
 
     def remote(src, dst, send, recv, pb=None, dev=None):
         return pltpu.make_async_remote_copy(
@@ -86,7 +97,8 @@
         )
 
     barrier = pltpu.get_barrier_semaphore()
-    for step in range(1, n_dev):
+    far_first = list(range(n_dev - 1, 0, -1))
+    for step in far_first:
         pl.semaphore_signal(
             barrier, inc=1, device_id=(my_pb, dev_mate(step)), device_id_type=MESH
         )
@@ -99,6 +111,9 @@
         pltpu.make_async_copy(queries, q_own, in_sem.at[0]),
         pltpu.make_async_copy(documents, d_own, in_sem.at[1]),
         pltpu.make_async_copy(normalizers, z_own, in_sem.at[2]),
+        pltpu.make_async_copy(lengths_in, lengths, in_sem.at[3]),
+        pltpu.make_async_copy(probs_in, probs, in_sem.at[4]),
+        pltpu.make_async_copy(positives_in, positives, in_sem.at[5]),
     ]
     for load in loads:
         load.start()
@@ -132,14 +147,14 @@
     pl.semaphore_wait(barrier, n_dev - 1 + n_pb - 1)
 
     aux_copies, q_copies, d_copies = [], [], []
-    for step in range(1, n_dev):
+    for step in far_first:
         mate = dev_mate(step)
         copy = remote(
             aux_send.at[mate], aux_recv.at[my_dev], a_ss.at[step], a_rs.at[step], dev=mate
         )
         copy.start()
         aux_copies.append(copy)
-    for step in range(1, n_dev):
+    for step in far_first:
         copy = remote(q_own, q_all.at[my_dev], q_ss.at[step], q_rs.at[step], dev=dev_mate(step))
         copy.start()
         q_copies.append(copy)
@@ -167,20 +182,22 @@
         copy.start()
         turn_copies.append(copy)
 
-    for copy in q_copies + d_copies + turn_copies:
+    for copy in q_copies + d_copies:
         copy.wait_recv()
 
     q_rows = q_all[...].reshape(n_dev * tokens, q_own.shape[1])
+
+    def score(p):
+        scores[p] = lax.dot_general(
+            d_all[p], q_rows, (((1,), (1,)), ((), ())), preferred_element_type=F32
+        )
 
     def interact(p, total):
         d_rows = d_all[p]
-        scores = lax.dot_general(
-            d_rows, q_rows, (((1,), (1,)), ((), ())), preferred_element_type=F32
-        )
         aux = aux_all[p]
         parts = []
         for k in range(own_docs):
-            shifted = sharpness * scores[k * slots : (k + 1) * slots, :] - aux[k : k + 1, :]
+            shifted = sharpness * scores[p, k * slots : (k + 1) * slots, :] - aux[k : k + 1, :]
             weight = jnp.exp(jnp.minimum(shifted, 0.0)) * aux[own_docs + k : own_docs + k + 1, :]
             parts.append(weight.astype(jnp.bfloat16))
         weight = jnp.concatenate(parts, axis=0)
@@ -204,21 +221,28 @@
         pair_copies.append(copy)
 
     if n_chip <= 2:
+        for step in range(0, n_pb):
+            score(pb_mate(step))
+        for copy in turn_copies:
+            copy.wait_recv()
+        total = interact(my_pb, total)
         for step in range(1, n_chip):
             for core in range(2):
                 total = interact(chip_mate(step) * 2 + core, total)
             send_pair(step)
-        for core in range(2):
-            total = interact(my_chip * 2 + core, total)
+        total = interact(partner, total)
         send_pair(0)
     else:
+        for copy in turn_copies:
+            copy.wait_recv()
+        lax.fori_loop(0, n_pb, lambda p, c: (score(p), c)[1], 0)
         total = lax.fori_loop(0, n_pb, interact, total)
         for step in list(range(1, n_chip)) + [0]:
             send_pair(step)
     q_part[...] = total.reshape(q_part.shape)
 
     out_copies = []
-    for step in range(1, n_dev):
+    for step in far_first:
         mate = dev_mate(step)
         copy = remote(q_part.at[mate], q_recv.at[my_dev], r_ss.at[step], r_rs.at[step], dev=mate)
         copy.start()
@@ -258,6 +282,17 @@
         aux_copies + q_copies + d_copies + turn_copies + pair_copies + out_copies + chip_copies
     ):
         copy.wait_send()
+
+
+def write_out(query_grad, doc_grad, query_out, doc_out, sem):
+    copies = [
+        pltpu.make_async_copy(query_grad, query_out, sem.at[0]),
+        pltpu.make_async_copy(doc_grad, doc_out, sem.at[1]),
+    ]
+    for copy in copies:
+        copy.start()
+    for copy in copies:
+        copy.wait()
 
 
 def per_device(queries, documents, lengths, normalizers, probs, positives):
@@ -271,16 +306,19 @@
     dma = pltpu.SemaphoreType.DMA
     hbm = pl.BlockSpec(memory_space=pl.ANY)
     vmem = pl.BlockSpec(memory_space=pltpu.VMEM)
-    smem = pl.BlockSpec(memory_space=pltpu.SMEM)
-    return pl.pallas_call(
+    grads = pl.pallas_call(
         functools.partial(kernel, n_pb, n_dev),
         out_shape=(
-            jax.ShapeDtypeStruct((tokens, width), F32),
-            jax.ShapeDtypeStruct((rows, width), F32),
+            pltpu.VMEM((tokens, width), F32),
+            pltpu.VMEM((rows, width), F32),
         ),
-        in_specs=[hbm, hbm, smem, hbm, vmem, smem],
+        in_specs=[hbm] * 6,
         out_specs=(vmem, vmem),
         scratch_shapes=[
+            pltpu.SMEM(lengths.shape, jnp.int32),
+            pltpu.VMEM(probs.shape, F32),
+            pltpu.SMEM(positives.shape, jnp.int32),
+            pltpu.VMEM((n_pb, rows, n_dev * tokens), F32),
             pltpu.VMEM((tokens, width), bf16),
             pltpu.VMEM((rows, width), bf16),
             pltpu.VMEM(normalizers.shape, F32),
@@ -296,7 +334,7 @@
             pltpu.VMEM((n_chip, rows, width), F32),
             pltpu.VMEM((n_dev, tokens, width), F32),
             pltpu.VMEM((n_dev, tokens, width), F32),
-            dma((3,)),
+            dma((6,)),
         ]
         + [dma((n_dev,))] * 4
         + [dma((n_pb,))] * 4
@@ -304,6 +342,16 @@
         + [dma((n_dev,))] * 2,
         compiler_params=pltpu.CompilerParams(collective_id=0, has_side_effects=True),
     )(queries, documents, lengths, normalizers, probs, positives)
+    return pl.pallas_call(
+        write_out,
+        out_shape=(
+            jax.ShapeDtypeStruct((tokens, width), F32),
+            jax.ShapeDtypeStruct((rows, width), F32),
+        ),
+        in_specs=[vmem, vmem],
+        out_specs=(hbm, hbm),
+        scratch_shapes=[dma((2,))],
+    )(*grads)
 
 
 def solution(mesh):

time: 24.8 us -> 23.5 us (0.948)
  local copies, waits for them, and re-layouts: 2.89 us -> 1.25 us
  Pallas kernels: 20.9 us -> 21.3 us
    unnamed x2 -> x4, local copies, waits for them, and re-layouts: 2.89 us -> 1.25 us
    pallas_call x1 -> x2, Pallas kernels: 20.9 us -> 21.3 us  [the longest x1 19.7 us: per_device(): pl.pallas_call(functools.partial(kernel, n_pb, n_dev), out_shape=(pltpu.V...]
where the time goes in v2:
time: 23.5 us; the launch traced here: 23.2 us
  Pallas kernels  21.3 us (91%)
  local copies, waits for them, and re-layouts  1.25 us (5%)
  between operations  0.65 us (3%)
    pallas_call x1, Pallas kernels, per_device(): pl.pallas_call(functools.partial(kernel, n_pb, n_dev), out_shape=(pltpu.V...  19.7 us
    pallas_call x1, Pallas kernels, per_device(): pl.pallas_call(write_out, out_shape=(jax.ShapeDtypeStruct((tokens, width)...  1.6 us
    unnamed x4, local copies, waits for them, and re-layouts  1.25 us

profile of v2, /device:TPU:0, one launch (start us, length us, event | category | flops | bytes accessed | tf_op | source)
XLA Modules:
  0.0 23.2 jit_solution(16166060045609012335)
XLA Ops:
  0.6 19.7 %shard_map.77 = (f32[32,128]{1,0:T(8,128)S(1)}, f32[256,128]{1,0:T(8,128)S(1)}) custom-call(bf16[32,128]{1,0:T(8,128)(2,1)} %queries.1, bf16[256,128]{1,0:T(8,128)(2,1)} %documents.1, s32[2]{0:T(128)} %lengths_in.1, f32[16,128]{1,0:T(8,128)} %normalizers.1, f32[4,16]{1,0:T(4,128)} %probs_in.1, s32[4]{0:T(128)} %positives_in.1), custom_call_target="tpu_custom_call" | custom-call | tf_op jit(solution)/shard_map/pallas_call | solution.py:309
  20.4 0.0 copy-start
  20.4 0.6 %copy-done = f32[256,128]{1,0:T(8,128)} copy-done((f32[256,128]{1,0:T(8,128)}, f32[256,128]{1,0:T(8,128)S(1)}, u32[]{:S(2)}) %copy-start) | copy-done | bytes 131096
  21.0 0.0 copy-start.1
  21.0 0.6 %copy-done.1 = f32[32,128]{1,0:T(8,128)} copy-done((f32[32,128]{1,0:T(8,128)}, f32[32,128]{1,0:T(8,128)S(1)}, u32[]{:S(2)}) %copy-start.1) | copy-done | bytes 16408
  21.6 1.6 %shard_map.78 = (f32[32,128]{1,0:T(8,128)}, f32[256,128]{1,0:T(8,128)}) custom-call(f32[32,128]{1,0:T(8,128)} %copy-done.1, f32[256,128]{1,0:T(8,128)} %copy-done), custom_call_target="tpu_custom_call" | custom-call | tf_op jit(solution)/shard_map/pallas_call | solution.py:345
Async XLA Ops:
  20.4 0.6 %copy-start = (f32[256,128]{1,0:T(8,128)}, f32[256,128]{1,0:T(8,128)S(1)}, u32[]{:S(2)}) copy-start(f32[256,128]{1,0:T(8,128)S(1)} %get-tuple-element.5.doc_grad) | copy-start | bytes 393220
  21.0 0.6 %copy-start.1 = (f32[32,128]{1,0:T(8,128)}, f32[32,128]{1,0:T(8,128)S(1)}, u32[]{:S(2)}) copy-start(f32[32,128]{1,0:T(8,128)S(1)} %get-tuple-element.4.query_grad) | copy-start | bytes 49156

commit v3 on v2

--- a/solution.py
+++ b/solution.py
@@ -284,17 +284,6 @@
         copy.wait_send()
 
 
-def write_out(query_grad, doc_grad, query_out, doc_out, sem):
-    copies = [
-        pltpu.make_async_copy(query_grad, query_out, sem.at[0]),
-        pltpu.make_async_copy(doc_grad, doc_out, sem.at[1]),
-    ]
-    for copy in copies:
-        copy.start()
-    for copy in copies:
-        copy.wait()
-
-
 def per_device(queries, documents, lengths, normalizers, probs, positives):
     n_pb, n_dev = lax.axis_size("pb"), lax.axis_size("dev")
     tokens, width = queries.shape
@@ -306,7 +295,7 @@
     dma = pltpu.SemaphoreType.DMA
     hbm = pl.BlockSpec(memory_space=pl.ANY)
     vmem = pl.BlockSpec(memory_space=pltpu.VMEM)
-    grads = pl.pallas_call(
+    return pl.pallas_call(
         functools.partial(kernel, n_pb, n_dev),
         out_shape=(
             pltpu.VMEM((tokens, width), F32),
@@ -342,16 +331,6 @@
         + [dma((n_dev,))] * 2,
         compiler_params=pltpu.CompilerParams(collective_id=0, has_side_effects=True),
     )(queries, documents, lengths, normalizers, probs, positives)
-    return pl.pallas_call(
-        write_out,
-        out_shape=(
-            jax.ShapeDtypeStruct((tokens, width), F32),
-            jax.ShapeDtypeStruct((rows, width), F32),
-        ),
-        in_specs=[vmem, vmem],
-        out_specs=(hbm, hbm),
-        scratch_shapes=[dma((2,))],
-    )(*grads)
 
 
 def solution(mesh):

time: 23.5 us -> 21.8 us (0.928)
  Pallas kernels: 21.3 us -> 19.7 us
    pallas_call x1 -> x0, Pallas kernels: 1.6 us -> none  [per_device(): pl.pallas_call(write_out, out_shape=(jax.ShapeDtypeStruct((tokens, width)...]
    unnamed x4 -> x2, local copies, waits for them, and re-layouts: 1.25 us -> 1.26 us
where the time goes in v3:
time: 21.8 us; the launch traced here: 21.6 us
  Pallas kernels  19.7 us (90%)
  local copies, waits for them, and re-layouts  1.26 us (6%)
  between operations  0.64 us (3%)
    pallas_call x1, Pallas kernels, per_device(): pl.pallas_call(functools.partial(kernel, n_pb, n_dev), out_shape=(pltpu.V...  19.7 us
    unnamed x2, local copies, waits for them, and re-layouts  1.26 us

profile of v3, /device:TPU:0, one launch (start us, length us, event | category | flops | bytes accessed | tf_op | source)
XLA Modules:
  0.0 21.6 jit_solution(11252756754399391699)
XLA Ops:
  0.6 19.7 %shard_map.77 = (f32[32,128]{1,0:T(8,128)S(1)}, f32[256,128]{1,0:T(8,128)S(1)}) custom-call(bf16[32,128]{1,0:T(8,128)(2,1)} %queries.1, bf16[256,128]{1,0:T(8,128)(2,1)} %documents.1, s32[2]{0:T(128)} %lengths_in.1, f32[16,128]{1,0:T(8,128)} %normalizers.1, f32[4,16]{1,0:T(4,128)} %probs_in.1, s32[4]{0:T(128)} %positives_in.1), custom_call_target="tpu_custom_call" | custom-call | tf_op jit(solution)/shard_map/pallas_call | solution.py:298
  20.4 0.6 %copy.10 = f32[32,128]{1,0:T(8,128)} copy(f32[32,128]{1,0:T(8,128)S(1)} %get-tuple-element.2) | data formatting | bytes 32768
  21.0 0.7 %copy.11 = f32[256,128]{1,0:T(8,128)} copy(f32[256,128]{1,0:T(8,128)S(1)} %get-tuple-element.3) | data formatting | bytes 262144

commit v4 on v3

--- a/solution.py
+++ b/solution.py
@@ -10,6 +10,18 @@
 sharpness = 10.0
 MESH = pl.DeviceIdType.MESH
 F32 = jnp.float32
+
+
+LEVELS = 32000.0
+
+
+def encode(part):
+    peak = jnp.maximum(jnp.max(jnp.abs(part), axis=1, keepdims=True), 1e-30)
+    return jnp.round(part * (LEVELS / peak)).astype(jnp.int32).astype(jnp.int16), peak
+
+
+def decode(code, peak):
+    return code.astype(jnp.int32).astype(F32) * (peak * (1.0 / LEVELS))
 
 
 def kernel(
@@ -38,10 +50,15 @@
     aux_all,
     doc_part,
     pair_recv,
-    pair_sum,
-    chip_recv,
+    pair_code,
+    pair_peak,
+    chip_code,
+    chip_peak,
     q_part,
+    q_code,
+    q_peak,
     q_recv,
+    q_recv_peak,
     in_sem,
     q_ss,
     q_rs,
@@ -57,6 +74,10 @@
     c_rs,
     r_ss,
     r_rs,
+    rp_ss,
+    rp_rs,
+    cp_ss,
+    cp_rs,
 ):
     my_pb = lax.axis_index("pb")
     my_dev = lax.axis_index("dev")
@@ -240,46 +261,60 @@
         for step in list(range(1, n_chip)) + [0]:
             send_pair(step)
     q_part[...] = total.reshape(q_part.shape)
-
-    out_copies = []
+    q_code[...], q_peak[...] = encode(total.reshape(q_part.shape))
+
+    out_copies, peak_copies = [], []
     for step in far_first:
         mate = dev_mate(step)
-        copy = remote(q_part.at[mate], q_recv.at[my_dev], r_ss.at[step], r_rs.at[step], dev=mate)
+        copy = remote(
+            q_peak.at[mate], q_recv_peak.at[my_dev], rp_ss.at[step], rp_rs.at[step], dev=mate
+        )
+        copy.start()
+        peak_copies.append(copy)
+        copy = remote(q_code.at[mate], q_recv.at[my_dev], r_ss.at[step], r_rs.at[step], dev=mate)
         copy.start()
         out_copies.append(copy)
-    q_recv[my_dev] = q_part[my_dev]
-
-    chip_copies = []
+
+    chip_copies, chip_peak_copies = [], []
     for step in range(1, n_chip):
         pair_copies[step - 1].wait_recv()
-        pair_sum[step] = doc_part[chip_mate(step) * 2 + my_core] + pair_recv[step]
-        copy = remote(
-            pair_sum.at[step],
-            chip_recv.at[step],
-            c_ss.at[step],
-            c_rs.at[step],
-            pb=chip_mate(step) * 2 + my_core,
+        mate = chip_mate(step) * 2 + my_core
+        pair_sum = doc_part[mate] + pair_recv[step]
+        pair_code[step], pair_peak[step] = encode(
+            pair_sum.reshape(own_docs, slots, pair_sum.shape[1])
+        )
+        copy = remote(
+            pair_peak.at[step], chip_peak.at[step], cp_ss.at[step], cp_rs.at[step], pb=mate
+        )
+        copy.start()
+        chip_peak_copies.append(copy)
+        copy = remote(
+            pair_code.at[step], chip_code.at[step], c_ss.at[step], c_rs.at[step], pb=mate
         )
         copy.start()
         chip_copies.append(copy)
     pair_copies[-1].wait_recv()
     doc_total = doc_part[my_pb] + pair_recv[0]
+    doc_total = doc_total.reshape(own_docs, slots, doc_total.shape[1])
     for step in range(1, n_chip):
         chip_copies[step - 1].wait_recv()
-        doc_total = doc_total + chip_recv[step]
+        chip_peak_copies[step - 1].wait_recv()
+        doc_total = doc_total + decode(chip_code[step], chip_peak[step])
     for k in range(own_docs):
         span = slice(k * slots, (k + 1) * slots)
-        doc_out[span, :] = jnp.where(slot < lengths[k], doc_total[span, :], 0.0)
-
-    for copy in out_copies:
+        doc_out[span, :] = jnp.where(slot < lengths[k], doc_total[k], 0.0)
+
+    query_total = q_part[my_dev]
+    for step, copy, peak_copy in reversed(list(zip(far_first, out_copies, peak_copies))):
         copy.wait_recv()
-    query_total = q_recv[0]
-    for e in range(1, n_dev):
-        query_total = query_total + q_recv[e]
+        peak_copy.wait_recv()
+        mate = dev_mate(step)
+        query_total = query_total + decode(q_recv[mate], q_recv_peak[mate])
     query_out[...] = query_total
 
     for copy in (
         aux_copies + q_copies + d_copies + turn_copies + pair_copies + out_copies + chip_copies
+        + peak_copies + chip_peak_copies
     ):
         copy.wait_send()
 
@@ -319,16 +354,22 @@
             pltpu.VMEM((n_pb, 2 * own_docs, n_dev * tokens), F32),
             pltpu.VMEM((n_pb, rows, width), F32),
             pltpu.VMEM((n_chip, rows, width), F32),
-            pltpu.VMEM((n_chip, rows, width), F32),
-            pltpu.VMEM((n_chip, rows, width), F32),
+            pltpu.VMEM((n_chip, own_docs, rows // own_docs, width), jnp.int16),
+            pltpu.VMEM((n_chip, own_docs, 1, width), F32),
+            pltpu.VMEM((n_chip, own_docs, rows // own_docs, width), jnp.int16),
+            pltpu.VMEM((n_chip, own_docs, 1, width), F32),
             pltpu.VMEM((n_dev, tokens, width), F32),
-            pltpu.VMEM((n_dev, tokens, width), F32),
+            pltpu.VMEM((n_dev, tokens, width), jnp.int16),
+            pltpu.VMEM((n_dev, 1, width), F32),
+            pltpu.VMEM((n_dev, tokens, width), jnp.int16),
+            pltpu.VMEM((n_dev, 1, width), F32),
             dma((6,)),
         ]
         + [dma((n_dev,))] * 4
         + [dma((n_pb,))] * 4
         + [dma((n_chip,))] * 4
-        + [dma((n_dev,))] * 2,
+        + [dma((n_dev,))] * 4
+        + [dma((n_chip,))] * 2,
         compiler_params=pltpu.CompilerParams(collective_id=0, has_side_effects=True),
     )(queries, documents, lengths, normalizers, probs, positives)
 

time: 21.8 us -> 20.9 us (0.959)
  Pallas kernels: 19.7 us -> 18.8 us
    pallas_call x1, Pallas kernels: 19.7 us -> 18.8 us  [per_device(): pl.pallas_call(functools.partial(kernel, n_pb, n_dev), out_shape=(pltpu.V...]
where the time goes in v4:
time: 20.9 us; the launch traced here: 20.7 us
  Pallas kernels  18.8 us (90%)
  local copies, waits for them, and re-layouts  1.26 us (6%)
  between operations  0.64 us (3%)
    pallas_call x1, Pallas kernels, per_device(): pl.pallas_call(functools.partial(kernel, n_pb, n_dev), out_shape=(pltpu.V...  18.8 us
    unnamed x2, local copies, waits for them, and re-layouts  1.26 us

profile of v4, /device:TPU:0, one launch (start us, length us, event | category | flops | bytes accessed | tf_op | source)
XLA Modules:
  0.0 20.7 jit_solution(10431262488262106245)
XLA Ops:
  0.6 18.8 %shard_map.77 = (f32[32,128]{1,0:T(8,128)S(1)}, f32[256,128]{1,0:T(8,128)S(1)}) custom-call(bf16[32,128]{1,0:T(8,128)(2,1)} %queries.1, bf16[256,128]{1,0:T(8,128)(2,1)} %documents.1, s32[2]{0:T(128)} %lengths_in.1, f32[16,128]{1,0:T(8,128)} %normalizers.1, f32[4,16]{1,0:T(4,128)} %probs_in.1, s32[4]{0:T(128)} %positives_in.1), custom_call_target="tpu_custom_call" | custom-call | tf_op jit(solution)/shard_map/pallas_call | solution.py:333
  19.4 0.6 %copy.10 = f32[32,128]{1,0:T(8,128)} copy(f32[32,128]{1,0:T(8,128)S(1)} %get-tuple-element.2) | data formatting | bytes 32768
  20.1 0.7 %copy.11 = f32[256,128]{1,0:T(8,128)} copy(f32[256,128]{1,0:T(8,128)S(1)} %get-tuple-element.3) | data formatting | bytes 262144

commit v5 on v4

--- a/solution.py
+++ b/solution.py
@@ -156,8 +156,8 @@
         span = slice(e * own_docs, (e + 1) * own_docs)
         aux_send[e, 0:own_docs, :] = z_own[span, :]
         aux_send[e, own_docs : 2 * own_docs, :] = signal[span, :]
-    aux_recv[my_dev] = aux_send[my_dev]
-    q_all[my_dev] = q_own[...]
+    aux_recv[0] = aux_send[my_dev]
+    q_all[0] = q_own[...]
 
     slot = lax.broadcasted_iota(jnp.int32, (slots, 1), 0)
     for k in range(own_docs):
@@ -171,12 +171,12 @@
     for step in far_first:
         mate = dev_mate(step)
         copy = remote(
-            aux_send.at[mate], aux_recv.at[my_dev], a_ss.at[step], a_rs.at[step], dev=mate
+            aux_send.at[mate], aux_recv.at[step], a_ss.at[step], a_rs.at[step], dev=mate
         )
         copy.start()
         aux_copies.append(copy)
     for step in far_first:
-        copy = remote(q_own, q_all.at[my_dev], q_ss.at[step], q_rs.at[step], dev=dev_mate(step))
+        copy = remote(q_own, q_all.at[step], q_ss.at[step], q_rs.at[step], dev=dev_mate(step))
         copy.start()
         q_copies.append(copy)
     for step in range(1, n_pb):
@@ -213,21 +213,25 @@
             d_all[p], q_rows, (((1,), (1,)), ((), ())), preferred_element_type=F32
         )
 
-    def interact(p, total):
+    half = n_dev // 2 * tokens
+
+    def interact(p, total, far):
+        span = slice(half, 2 * half) if far else slice(0, half)
         d_rows = d_all[p]
         aux = aux_all[p]
         parts = []
         for k in range(own_docs):
-            shifted = sharpness * scores[p, k * slots : (k + 1) * slots, :] - aux[k : k + 1, :]
-            weight = jnp.exp(jnp.minimum(shifted, 0.0)) * aux[own_docs + k : own_docs + k + 1, :]
+            shifted = sharpness * scores[p, k * slots : (k + 1) * slots, span] - aux[k : k + 1, span]
+            weight = jnp.exp(jnp.minimum(shifted, 0.0)) * aux[own_docs + k : own_docs + k + 1, span]
             parts.append(weight.astype(jnp.bfloat16))
         weight = jnp.concatenate(parts, axis=0)
-        doc_part[p] = jnp.dot(weight, q_rows, preferred_element_type=F32)
+        part = jnp.dot(weight, q_rows[span, :], preferred_element_type=F32)
+        doc_part[p] = part if far else doc_part[p] + part
         return total + lax.dot_general(
             weight, d_rows, (((0,), (0,)), ((), ())), preferred_element_type=F32
         )
 
-    total = jnp.zeros((n_dev * tokens, q_own.shape[1]), F32)
+    zero = jnp.zeros((half, q_own.shape[1]), F32)
     pair_copies = []
 
     def send_pair(step):
@@ -241,39 +245,53 @@
         copy.start()
         pair_copies.append(copy)
 
+    out_copies, peak_copies = [], []
+
+    def send_half(total, far):
+        first = n_dev // 2 if far else 0
+        rows = total.reshape(n_dev // 2, tokens, total.shape[1])
+        span = slice(first, first + n_dev // 2)
+        if not far:
+            q_part[...] = rows[0]
+        q_code[span], q_peak[span] = encode(rows)
+        for step in range(first + n_dev // 2 - 1, max(first, 1) - 1, -1):
+            mate = dev_mate(step)
+            copy = remote(
+                q_peak.at[step], q_recv_peak.at[step], rp_ss.at[step], rp_rs.at[step], dev=mate
+            )
+            copy.start()
+            peak_copies.append(copy)
+            copy = remote(q_code.at[step], q_recv.at[step], r_ss.at[step], r_rs.at[step], dev=mate)
+            copy.start()
+            out_copies.append(copy)
+
     if n_chip <= 2:
         for step in range(0, n_pb):
             score(pb_mate(step))
         for copy in turn_copies:
             copy.wait_recv()
-        total = interact(my_pb, total)
+        total = zero
+        for step in range(n_pb - 1, -1, -1):
+            total = interact(pb_mate(step), total, True)
+        send_half(total, True)
+        total = zero
         for step in range(1, n_chip):
             for core in range(2):
-                total = interact(chip_mate(step) * 2 + core, total)
+                total = interact(chip_mate(step) * 2 + core, total, False)
             send_pair(step)
-        total = interact(partner, total)
+        total = interact(partner, total, False)
         send_pair(0)
+        total = interact(my_pb, total, False)
     else:
         for copy in turn_copies:
             copy.wait_recv()
         lax.fori_loop(0, n_pb, lambda p, c: (score(p), c)[1], 0)
-        total = lax.fori_loop(0, n_pb, interact, total)
+        total = lax.fori_loop(0, n_pb, lambda p, c: interact(p, c, True), zero)
+        send_half(total, True)
+        total = lax.fori_loop(0, n_pb, lambda p, c: interact(p, c, False), zero)
         for step in list(range(1, n_chip)) + [0]:
             send_pair(step)
-    q_part[...] = total.reshape(q_part.shape)
-    q_code[...], q_peak[...] = encode(total.reshape(q_part.shape))
-
-    out_copies, peak_copies = [], []
-    for step in far_first:
-        mate = dev_mate(step)
-        copy = remote(
-            q_peak.at[mate], q_recv_peak.at[my_dev], rp_ss.at[step], rp_rs.at[step], dev=mate
-        )
-        copy.start()
-        peak_copies.append(copy)
-        copy = remote(q_code.at[mate], q_recv.at[my_dev], r_ss.at[step], r_rs.at[step], dev=mate)
-        copy.start()
-        out_copies.append(copy)
+    send_half(total, False)
 
     chip_copies, chip_peak_copies = [], []
     for step in range(1, n_chip):
@@ -304,12 +322,11 @@
         span = slice(k * slots, (k + 1) * slots)
         doc_out[span, :] = jnp.where(slot < lengths[k], doc_total[k], 0.0)
 
-    query_total = q_part[my_dev]
+    query_total = q_part[...]
     for step, copy, peak_copy in reversed(list(zip(far_first, out_copies, peak_copies))):
         copy.wait_recv()
         peak_copy.wait_recv()
-        mate = dev_mate(step)
-        query_total = query_total + decode(q_recv[mate], q_recv_peak[mate])
+        query_total = query_total + decode(q_recv[step], q_recv_peak[step])
     query_out[...] = query_total
 
     for copy in (
@@ -358,7 +375,7 @@
             pltpu.VMEM((n_chip, own_docs, 1, width), F32),
             pltpu.VMEM((n_chip, own_docs, rows // own_docs, width), jnp.int16),
             pltpu.VMEM((n_chip, own_docs, 1, width), F32),
-            pltpu.VMEM((n_dev, tokens, width), F32),
+            pltpu.VMEM((tokens, width), F32),
             pltpu.VMEM((n_dev, tokens, width), jnp.int16),
             pltpu.VMEM((n_dev, 1, width), F32),
             pltpu.VMEM((n_dev, tokens, width), jnp.int16),

time: 20.9 us -> 20.6 us (0.986)
  Pallas kernels: 18.8 us -> 18.5 us
    pallas_call x1, Pallas kernels: 18.8 us -> 18.5 us  [per_device(): pl.pallas_call(functools.partial(kernel, n_pb, n_dev), out_shape=(pltpu.V...]
where the time goes in v5:
time: 20.6 us; the launch traced here: 20.4 us
  Pallas kernels  18.5 us (90%)
  local copies, waits for them, and re-layouts  1.26 us (6%)
  between operations  0.64 us (3%)
    pallas_call x1, Pallas kernels, per_device(): pl.pallas_call(functools.partial(kernel, n_pb, n_dev), out_shape=(pltpu.V...  18.5 us
    unnamed x2, local copies, waits for them, and re-layouts  1.26 us

profile of v5, /device:TPU:0, one launch (start us, length us, event | category | flops | bytes accessed | tf_op | source)
XLA Modules:
  0.0 20.4 jit_solution(1392537761937932640)
XLA Ops:
  0.6 18.5 %shard_map.77 = (f32[32,128]{1,0:T(8,128)S(1)}, f32[256,128]{1,0:T(8,128)S(1)}) custom-call(bf16[32,128]{1,0:T(8,128)(2,1)} %queries.1, bf16[256,128]{1,0:T(8,128)(2,1)} %documents.1, s32[2]{0:T(128)} %lengths_in.1, f32[16,128]{1,0:T(8,128)} %normalizers.1, f32[4,16]{1,0:T(4,128)} %probs_in.1, s32[4]{0:T(128)} %positives_in.1), custom_call_target="tpu_custom_call" | custom-call | tf_op jit(solution)/shard_map/pallas_call | solution.py:350
  19.1 0.6 %copy.10 = f32[32,128]{1,0:T(8,128)} copy(f32[32,128]{1,0:T(8,128)S(1)} %get-tuple-element.2) | data formatting | bytes 32768
  19.7 0.7 %copy.11 = f32[256,128]{1,0:T(8,128)} copy(f32[256,128]{1,0:T(8,128)S(1)} %get-tuple-element.3) | data formatting | bytes 262144
